TPU v7x, 512 devices: a whole 4x8x8 slice. The times are simulated.
512 devices in a mesh: gx: 4 (over y_hi), gy: 16 (over z, y_lo), gz: 8 (over x, core).
Axes of the slice: x: 4, y: 8 (y_hi: 4, y_lo: 2; y = y_hi * 2 + y_lo), z: 8, core: 2. Of those that a mesh axis runs over, the one named last changes fastest.
Arguments:
- nodal_scalar_values: float32 [3, 32, 128, 16384], P(None, 'gx', 'gy', 'gz'), may hold values from -6 to 6
- geometry: float32 [6, 4, 16, 2048], P(None, 'gx', 'gy', 'gz'), may hold values from -1.2 to 4, as said below
Outputs:
- assembled: float32 [3, 32, 128, 16384], P(None, 'gx', 'gy', 'gz')
Inputs may be any that keep to these rules, and one draw needn't show every extreme that they name: `geometry`: G00, G11 and G22 are positive; each off-diagonal factor is at most 0.3 times the root of the product of its two diagonal factors in magnitude.
All inputs are finite; a program needn't handle non-finite values.
Results may differ from a plain program's by a relative error of at most 0.00007.
Values sent between devices are 32-bit elements; how exact they have to be, the bound alone decides.
No kernel may reach another device: no remote copies, remote signals or barrier semaphores. Data moves between devices by JAX's collectives and lax.ppermute only.
A program may use at most 64 MiB of HBM per device.

v0:
```python
import jax
import jax.numpy as jnp
import numpy as np
from jax import lax
from jax.experimental import pallas as pl
from jax.experimental.pallas import tpu as pltpu
from jax.sharding import PartitionSpec as P


interior_points = [
    -0.8717401485096066,
    -0.5917001814331423,
    -0.2092992179024789,
    0.2092992179024789,
    0.5917001814331423,
    0.8717401485096066,
]
LANES = 128
COMPONENTS = 3
BLOCK = 256
F32 = jnp.float32
BF16 = jnp.bfloat16


def legendre_seven(point):
    previous = 1.0
    current = point
    for order in range(1, 7):
        following = ((2 * order + 1) * point * current - order * previous) / (order + 1)
        previous = current
        current = following
    return current


def gll_tables():
    degree = 7
    points = [-1.0] + interior_points + [1.0]
    values = [legendre_seven(point) for point in points]
    node_count = degree + 1
    weights = np.array([2.0 / (degree * (degree + 1) * value * value) for value in values])
    derivative = np.zeros((node_count, node_count))
    for row_index in range(node_count):
        for col_index in range(node_count):
            if row_index != col_index:
                derivative[row_index, col_index] = values[row_index] / (
                    values[col_index] * (points[row_index] - points[col_index])
                )
    derivative[0, 0] = -degree * (degree + 1) / 4.0
    derivative[node_count - 1, node_count - 1] = degree * (degree + 1) / 4.0
    return (derivative.astype(np.float32).astype(np.float64), weights)


def split_table(table):
    high = np.asarray(table, np.float32).astype(jnp.bfloat16)
    low = (np.asarray(table, np.float64) - high.astype(np.float64)).astype(jnp.bfloat16)
    return high, low


def tables():
    derivative, weights = gll_tables()
    eye = np.eye(8)

    def doubled(table):
        high, low = split_table(table)
        top = np.concatenate([high, high], 1)
        return np.concatenate([top, np.concatenate([low, np.zeros_like(low)], 1)], 0)

    high, low = split_table(np.concatenate([np.kron(derivative, eye), np.kron(eye, derivative)], 0))
    grad_y = np.concatenate([high, high, low], 1)
    back = (derivative * weights[:, None]).T
    both = np.concatenate([np.kron(back, np.diag(weights)), np.kron(np.diag(weights), back)], 1)
    back_y = doubled(both)
    many = np.eye(LANES // 8)

    def stacked(table):
        high, low = split_table(table)
        bottom = np.concatenate([high, np.zeros_like(low)], 1)
        return np.concatenate([np.concatenate([high, low], 1), bottom], 0)

    grad_z = stacked(np.kron(many, derivative.T))
    back_z = stacked(np.kron(many, derivative))
    spread = np.kron(np.eye(LANES)[:, : BLOCK // 8], np.ones((1, 8))).astype(jnp.bfloat16)
    weight_z = np.tile(weights, BLOCK // 8)[None].astype(np.float32)
    plane = np.tile(np.kron(weights, weights)[:, None], (1, BLOCK)).astype(np.float32)
    return grad_y, back_y, grad_z, back_z, spread, weight_z, plane


def split(values):
    high = values.astype(BF16)
    return high, (values - high.astype(F32)).astype(BF16)


def dot(left, right):
    return jnp.dot(left, right, preferred_element_type=F32)


def lane_iota():
    return lax.broadcasted_iota(jnp.int32, (8, LANES), 1)


def along_z(high, low, table):
    rows, width = high.shape
    halves = []
    for k in range(width // LANES):
        lanes = slice(k * LANES, k * LANES + LANES)
        halves.append(jnp.concatenate([high[:, lanes], low[:, lanes]], 1))
    both = dot(jnp.concatenate(halves, 0), table)
    both = both[:, :LANES] + both[:, LANES:]
    return jnp.concatenate([both[k * rows : k * rows + rows] for k in range(width // LANES)], 1)


def operator_block(field, factor, gxy_ref, bxy_ref, gz_ref, bz_ref, plane):
    count = field.shape[0] // 64
    high, low = split(field)
    grad_z = along_z(high, low, gz_ref[...])
    g = [factor[k : k + 1] for k in range(6)]
    fluxes = []
    sums = []
    for c in range(count):
        mine = slice(64 * c, 64 * c + 64)
        both = dot(gxy_ref[...], jnp.concatenate([high[mine], low[mine], high[mine]], 0))
        gx, gy = both[:64], both[64:]
        gz = grad_z[mine]
        fx = g[0] * gx + g[3] * gy + g[4] * gz
        fy = g[3] * gx + g[1] * gy + g[5] * gz
        fz = g[4] * gx + g[5] * gy + g[2] * gz
        fluxes.append(fz)
        fh, fl = split(jnp.concatenate([fx, fy], 0))
        both = dot(bxy_ref[...], jnp.concatenate([fh, fl], 0))
        sums.append(both[:64] + both[64:])
    fh, fl = split(jnp.concatenate(fluxes, 0))
    back = along_z(fh, fl, bz_ref[...])
    return [sums[c] + plane * back[64 * c : 64 * c + 64] for c in range(count)]


def spread_rows(rows, spread, weight):
    first = rows.astype(BF16)
    rest = rows - first.astype(F32)
    second = rest.astype(BF16)
    third = (rest - second.astype(F32)).astype(BF16)
    return (dot(first, spread) + dot(second, spread) + dot(third, spread)) * weight


def load_kernel(
    u_hbm, geo_hbm, gy_hbm, by_hbm, gz_hbm, bz_hbm, spread_hbm, wz_hbm, plane_hbm,
    u_ref, factor_ref, gy_ref, by_ref, gz_ref, bz_ref, plane_ref, za_ref, zb_ref,
    geo_ref, spread_ref, wz_ref, sems,
):
    components = u_ref.shape[0]
    length = u_ref.shape[3]
    blocks = length // BLOCK
    per_block = BLOCK // 8
    copies = []
    ends = (pl.ds(0, LANES), pl.ds(length - LANES, LANES))
    middle = pl.ds(LANES, length - 2 * LANES)
    pairs = [(geo_hbm, geo_ref), (spread_hbm, spread_ref), (wz_hbm, wz_ref)]
    pairs += [(u_hbm.at[:, :, :, where], u_ref.at[:, :, :, where]) for where in ends]
    pairs += [(gz_hbm, gz_ref), (gy_hbm, gy_ref), (by_hbm, by_ref), (bz_hbm, bz_ref)]
    pairs += [(plane_hbm, plane_ref)]
    pairs += [(u_hbm.at[c, :, :, middle], u_ref.at[c, :, :, middle]) for c in range(components)]
    for k, (source, target) in enumerate(pairs):
        copies.append(pltpu.make_async_copy(source, target, sems.at[k]))
        copies[-1].start()
    for copy in copies[:3]:
        copy.wait()
    geo = jnp.concatenate(
        [geo_ref[k, 0] for k in range(6)] + [jnp.zeros((2, length // 8), F32)], 0
    )
    rows = []
    for block in range(blocks):
        start = block * per_block
        tile = geo[:, start // LANES * LANES : start // LANES * LANES + LANES]
        shift = start % LANES
        rows.append(pltpu.roll(tile, LANES - shift, 1) if shift else tile)
    expanded = spread_rows(jnp.concatenate(rows, 0), spread_ref[...], wz_ref[...])
    factor_ref[...] = expanded
    for copy in copies[3:10]:
        copy.wait()
    lower = lane_iota() < LANES // 2
    factor = jnp.where(lower, expanded[:8, :LANES], expanded[8 * blocks - 8 :, LANES:])
    lower = lax.broadcasted_iota(jnp.int32, (64, LANES), 1) < LANES // 2
    sides = []
    for c in range(components):
        begin, end = [u_ref[c, :, :, where].reshape(64, LANES) for where in ends]
        sides.append(jnp.where(lower, begin, end))
    totals = operator_block(
        jnp.concatenate(sides, 0), factor, gy_ref, by_ref, gz_ref, bz_ref, plane_ref[:, :LANES]
    )
    even_z = lax.rem(lax.axis_index("gz"), 2) == 0
    lane = lane_iota()
    low_plane = jnp.zeros((8, LANES), F32)
    high_plane = jnp.zeros((8, LANES), F32)
    for c in range(components):
        for x in range(8):
            slot = 8 * c + x
            both = totals[c][8 * x : 8 * x + 8]
            begin = pltpu.roll(both, slot, 1) if slot else both
            end = pltpu.roll(both, slot + 1, 1)
            low_plane = jnp.where(lane == slot, begin, low_plane)
            high_plane = jnp.where(lane == slot, end, high_plane)
    za_ref[...] = jnp.where(even_z, high_plane, low_plane)
    zb_ref[...] = jnp.where(even_z, low_plane, high_plane)
    for copy in copies[10:]:
        copy.wait()


def stiffness_kernel(
    u_ref, factor_ref, gy_ref, by_ref, gz_ref, bz_ref, plane_ref, out_ref
):
    components = u_ref.shape[0]
    blocks = u_ref.shape[3] // BLOCK
    tiles = blocks * (BLOCK // LANES)
    lane = lax.broadcasted_iota(jnp.int32, (64, LANES), 1)
    last, initial = lane % 8 == 7, lane % 8 == 0
    final_lane, first_lane = lane == LANES - 1, lane == 0
    zero = jnp.zeros((64, LANES), F32)
    plane = plane_ref[...]
    pending = [None] * components
    edge = [zero] * components

    def finish(c, tile, following):
        value, after, before, previous = pending[c]
        after = jnp.where(final_lane, following, after)
        before = jnp.where(first_lane, previous, before)
        change = jnp.where(last, after, jnp.where(initial, before, 0.0))
        out_ref[c * tiles + tile] = value + change

    for block in range(blocks):
        where = slice(block * BLOCK, block * BLOCK + BLOCK)
        field = jnp.concatenate(
            [u_ref[c, :, :, where].reshape(64, BLOCK) for c in range(components)], 0
        )
        factor = factor_ref[8 * block : 8 * block + 8, :]
        totals = operator_block(field, factor, gy_ref, by_ref, gz_ref, bz_ref, plane)
        for c in range(components):
            for k in range(BLOCK // LANES):
                value = totals[c][:, k * LANES : k * LANES + LANES]
                after = pltpu.roll(value, LANES - 1, 1)
                before = pltpu.roll(value, 1, 1)
                tile = block * (BLOCK // LANES) + k
                if tile:
                    finish(c, tile - 1, after)
                pending[c] = (value, after, before, edge[c])
                edge[c] = before
    for c in range(components):
        finish(c, tiles - 1, zero)


def ordered(even, first, second):
    return jnp.where(even, second, first), jnp.where(even, first, second)


def parities():
    x, y, z = [lax.axis_index(axis) for axis in ("gx", "gy", "gz")]
    return [lax.rem(index, 2) == 0 for index in (x + z, y, z)]


def at_lane(packed, slot, lane_to):
    shift = (lane_to - slot) % LANES
    moved = pltpu.roll(packed, shift, 1) if shift else packed
    return jnp.where(lane_iota() == lane_to, moved, 0.0)


def face_kernel(
    local_ref, za_ref, zb_ref, xa_ref, xb_ref, ia_ref, ea_ref, yb_ref, ends_ref
):
    tiles = local_ref.shape[0] // COMPONENTS
    even_x, even_y, even_z = parities()
    low, high = ordered(even_z, za_ref[...], zb_ref[...])
    for c in range(COMPONENTS):
        for k, (t, packed, lane_to) in enumerate(((0, low, 0), (tiles - 1, high, LANES - 1))):
            for x in range(8):
                rows = slice(8 * x, 8 * x + 8)
                halo = at_lane(packed, 8 * c + x, lane_to)
                ends_ref[2 * c + k, rows] = local_ref[c * tiles + t, rows] + halo

    for c in range(COMPONENTS):
        for t in range(tiles):
            spot = c * tiles + t
            ref, at = local_ref, spot
            if t in (0, tiles - 1):
                ref, at = ends_ref, 2 * c + (t > 0)
            first_plane = ref[at, 0:8]
            last_plane = ref[at, 56:64]
            xa_ref[spot] = jnp.where(even_x, last_plane, first_plane)
            xb_ref[spot] = jnp.where(even_x, first_plane, last_plane)
            first_rows = ref[at, pl.ds(0, 8, stride=8)]
            last_rows = ref[at, pl.ds(7, 8, stride=8)]
            rows_a = jnp.where(even_y, last_rows, first_rows)
            yb_ref[spot] = jnp.where(even_y, first_rows, last_rows)
            ia_ref[18 * t + 6 * c : 18 * t + 6 * c + 6] = rows_a[1:7]
            ea_ref[6 * t + 2 * c : 6 * t + 2 * c + 1] = rows_a[0:1]
            ea_ref[6 * t + 2 * c + 1 : 6 * t + 2 * c + 2] = rows_a[7:8]


def copy_kernel(in_ref, out_ref):
    out_ref[...] = in_ref[...]


def edge_kernel(ea_ref, yb_ref, xa_ref, xb_ref, outa_ref, outb_ref):
    tiles = ea_ref.shape[0] // 6
    components = xa_ref.shape[0] // tiles
    even_x, even_y, _ = parities()
    for c in range(components):
        for t in range(tiles):
            spot = c * tiles + t
            sides = ordered(even_x, xa_ref[spot], xb_ref[spot])
            outb_ref[spot] = yb_ref[spot]
            for k in range(2):
                at = 6 * t + 2 * c + k
                at = slice(at, at + 1)
                first, last = sides[k][0:1], sides[k][7:8]
                outa_ref[at] = ea_ref[at] + jnp.where(even_y, last, first)
                x = slice(7 * k, 7 * k + 1)
                outb_ref[spot, x] = yb_ref[spot, x] + jnp.where(even_y, first, last)


def base_kernel(
    local_ref, za_ref, zb_ref, xa_ref, xb_ref, out_hbm, first_ref, last_ref, out_ref, tile_ref, sems
):
    tiles = local_ref.shape[0] // COMPONENTS
    even_x, _, even_z = parities()
    low, high = ordered(even_z, za_ref[...], zb_ref[...])
    copies = []
    for c in range(COMPONENTS):
        for t in range(tiles):
            where = slice(t * LANES, t * LANES + LANES)
            spot = c * tiles + t
            planes = ordered(even_x, xa_ref[spot], xb_ref[spot])
            for x in range(8):
                value = local_ref[spot, 8 * x : 8 * x + 8]
                if t == 0:
                    value = value + at_lane(low, 8 * c + x, 0)
                if t == tiles - 1:
                    value = value + at_lane(high, 8 * c + x, LANES - 1)
                if x in (0, 7):
                    value = value + planes[x // 7]
                out_ref[c, x, :, where] = value
                tile_ref[spot, 8 * x : 8 * x + 8] = value
            first_ref[spot] = tile_ref[spot, pl.ds(0, 8, stride=8)]
            last_ref[spot] = tile_ref[spot, pl.ds(7, 8, stride=8)]
        copies.append(pltpu.make_async_copy(out_ref.at[c], out_hbm.at[c], sems.at[c]))
        copies[-1].start()
    for copy in copies:
        copy.wait()


def late_kernel(
    base_hbm, first_ref, last_ref, ia_ref, ea_ref, yb_ref, out_hbm, rows_ref, sems
):
    del base_hbm
    tiles = first_ref.shape[0] // COMPONENTS
    _, even_y, _ = parities()
    copies = []
    for c in range(COMPONENTS):
        for t in range(tiles):
            where = slice(t * LANES, t * LANES + LANES)
            spot = c * tiles + t
            outer = ea_ref[6 * t + 2 * c : 6 * t + 2 * c + 2]
            inner = ia_ref[18 * t + 6 * c : 18 * t + 6 * c + 6]
            side = jnp.concatenate([outer[0:1], inner, outer[1:2]], 0)
            front, behind = ordered(even_y, side, yb_ref[spot])
            rows_ref[c, 0, :, where] = first_ref[spot] + front
            rows_ref[c, 1, :, where] = last_ref[spot] + behind
        for k in range(2):
            copies.append(
                pltpu.make_async_copy(
                    rows_ref.at[c, k], out_hbm.at[c, :, 7 * k, :], sems.at[2 * c + k]
                )
            )
            copies[-1].start()
    for copy in copies:
        copy.wait()


def pairs_from(start, count):
    found = []
    for i in range(start, count - 1, 2):
        found += [(i, i + 1), (i + 1, i)]
    return found


def exchange(array, axis, start):
    return lax.ppermute(array, axis, pairs_from(start, lax.axis_size(axis)))


def mixed_exchange(array, side):
    width, height, depth = [lax.axis_size(axis) for axis in ("gx", "gy", "gz")]
    found = []
    for y in range(height):
        for z in range(depth):
            for i, j in pairs_from((side + z) % 2, width):
                found.append(((i * height + y) * depth + z, (j * height + y) * depth + z))
    return lax.ppermute(array, ("gx", "gy", "gz"), found)


def call(kernel, outs, scratch=(), flops=1000000, **specs):
    shapes = [out if hasattr(out, "dtype") else jax.ShapeDtypeStruct(out, F32) for out in outs]
    return pl.pallas_call(
        kernel,
        out_shape=shapes,
        scratch_shapes=list(scratch),
        compiler_params=pltpu.CompilerParams(vmem_limit_bytes=24 * 1024 * 1024),
        cost_estimate=pl.CostEstimate(flops=flops, bytes_accessed=1000000, transcendentals=0),
        **specs,
    )


def local(nodal, geometry):
    components, _, _, length = nodal.shape
    tiles = length // LANES
    blocks = length // BLOCK
    face = (components * tiles, 8, LANES)
    inner = (components * tiles * 6, LANES)
    edge = (components * tiles * 2, LANES)
    tile = (8, LANES)
    flat = (components * tiles, 64, LANES)
    constants = [jnp.asarray(table) for table in tables()]
    operands = [
        pltpu.with_memory_space_constraint(operand, pltpu.HBM)
        for operand in [nodal, geometry] + constants
    ]
    hbm = pl.BlockSpec(memory_space=pltpu.HBM)
    kept = [jax.ShapeDtypeStruct(constants[k].shape, constants[k].dtype) for k in (0, 1, 2, 3, 6)]
    loaded = call(
        load_kernel,
        [nodal.shape, (8 * blocks, BLOCK)] + kept + [tile, tile],
        [pltpu.VMEM(operands[k].shape, operands[k].dtype) for k in (1, 6, 7)]
        + [pltpu.SemaphoreType.DMA((10 + components,))],
        in_specs=[hbm] * len(operands),
    )(*operands)
    za = exchange(loaded[-2], "gz", 0)
    zb = exchange(loaded[-1], "gz", 1)
    (result,) = call(stiffness_kernel, [flat])(*loaded[:-2])
    xa, xb, ia, ea, yb = call(
        face_kernel,
        [face, face, inner, edge, face],
        [pltpu.VMEM((2 * components, 64, LANES), F32)],
    )(result, za, zb)
    xa = mixed_exchange(xa, 0)
    xb = mixed_exchange(xb, 1)
    ia = exchange(ia, "gy", 0)
    (ea,) = call(copy_kernel, [edge])(ea)
    ea, yb = call(edge_kernel, [edge, face])(ea, yb, xa, xb)
    yb = exchange(yb, "gy", 1)
    ea = exchange(ea, "gy", 0)
    vmem = pl.BlockSpec(memory_space=pltpu.VMEM)
    result, first, last = call(
        base_kernel,
        [nodal.shape, face, face],
        [
            pltpu.VMEM(nodal.shape, F32),
            pltpu.VMEM(flat, F32),
            pltpu.SemaphoreType.DMA((components,)),
        ],
        out_specs=[hbm, vmem, vmem],
    )(result, za, zb, xa, xb)
    (result,) = call(
        late_kernel,
        [nodal.shape],
        [pltpu.VMEM((components, 2, 8, length), F32), pltpu.SemaphoreType.DMA((2 * components,))],
        in_specs=[hbm] + [vmem] * 5,
        out_specs=[hbm],
        input_output_aliases={0: 0},
    )(result, first, last, ia, ea, yb)
    return result


def solution(mesh):
    return jax.shard_map(
        local,
        mesh=mesh,
        in_specs=(P(None, "gx", "gy", "gz"), P(None, "gx", "gy", "gz")),
        out_specs=P(None, "gx", "gy", "gz"),
        check_vma=False,
    )
```

profile of v0, /device:TPU:208, one launch (start us, length us, event | category | flops | bytes accessed | tf_op | source)
XLA Modules:
  0.0 42.1 jit_solution(4965193349750434576)
XLA Ops:
  0.0 1.8 %shard_map.91 = (f32[3,8,8,2048]{3,2,1,0:T(8,128)S(1)}, f32[64,256]{1,0:T(8,128)S(1)}, bf16[128,192]{1,0:T(8,128)(2,1)S(1)}, bf16[128,256]{1,0:T(8,128)(2,1)S(1)...) custom-call(f32[3,8,8,2048]{3,2,1,0:T(8,128)} %u_hbm.1, ...), custom_call_target="tpu_custom_call" | custom-call | flops 1000000 | bytes 1000000 | tf_op jit(solution)/shard_map/pallas_call | solution.py:425
  1.8 1.9 %collective-permute-start = (f32[8,128]{1,0:T(8,128)S(1)}, f32[8,128]{1,0:T(8,128)S(1)}, u32[]{:S(2)}, u32[]{:S(2)}) collective-permute-start(f32[8,128]{1,0:T(8,128)S(1)} %get-tuple-element.31), channel_id=1, source_target_pairs={{0,1},{1,0},{2,3},{3,2},{4,5},{5,4},{6,7},{7,6},{8,9},{9,8},{10,11... | collective-permute-start | bytes 12296 | tf_op jit(solution)/shard_map/ppermute | solution.py:384
  3.8 0.7 %collective-permute-start.1 = (f32[8,128]{1,0:T(8,128)S(1)}, f32[8,128]{1,0:T(8,128)S(1)}, u32[]{:S(2)}, u32[]{:S(2)}) collective-permute-start(f32[8,128]{1,0:T(8,128)S(1)} %get-tuple-element.32), channel_id=1, source_target_pairs={{1,2},{2,1},{3,4},{4,3},{5,6},{6,5},{9,10},{10,9},{11,12},{12,11},... | collective-permute-start | bytes 12296 | tf_op jit(solution)/shard_map/ppermute | solution.py:384
  4.4 3.4 %shard_map.92.local_ref = f32[48,64,128]{2,1,0:T(8,128)S(1)} custom-call(f32[3,8,8,2048]{3,2,1,0:T(8,128)S(1)} %get-tuple-element.24.u_ref, f32[64,256]{1,0:T(8,128)S(1)} %get-tuple-element.25.factor_ref, bf16[128,192]{1,0:T(8,128)(2,1)S(1)} %get-tuple-element.26.gy_ref, bf16[128,256]{1,0:T(8,128)(2,1)S(1)} %get-tuple-element.27.by_ref, ...), custom_call_target="tpu_custom_call" | custom-call | flops 1000000 | bytes 1000000 | tf_op jit(solution)/shard_map/pallas_call | solution.py:434
  7.9 0.0 collective-permute-done.za_ref
  7.9 0.0 collective-permute-done.1.zb_ref
  7.9 0.2 shard_map.93
  8.0 2.2 %collective-permute-start.2 = (f32[48,8,128]{2,1,0:T(8,128)S(1)}, f32[48,8,128]{2,1,0:T(8,128)S(1)}, u32[]{:S(2)}, u32[]{:S(2)}) collective-permute-start(f32[48,8,128]{2,1,0:T(8,128)S(1)} %get-tuple-element.33), channel_id=1, source_target_pairs={{0,128},{128,0},{256,384},{384,256},{129,257},{257,129},{2,130},{1... | collective-permute-start | bytes 589832 | tf_op jit(solution)/shard_map/ppermute | solution.py:394
  10.3 6.2 %collective-permute-start.3 = (f32[48,8,128]{2,1,0:T(8,128)S(1)}, f32[48,8,128]{2,1,0:T(8,128)S(1)}, u32[]{:S(2)}, u32[]{:S(2)}) collective-permute-start(f32[48,8,128]{2,1,0:T(8,128)S(1)} %get-tuple-element.34), channel_id=1, source_target_pairs={{128,256},{256,128},{1,129},{129,1},{257,385},{385,257},{130,258},... | collective-permute-start | bytes 589832 | tf_op jit(solution)/shard_map/ppermute | solution.py:394
  16.5 0.1 collective-permute-done.2.xa_ref
  16.6 8.8 %collective-permute-done.3.xb_ref = f32[48,8,128]{2,1,0:T(8,128)S(1)} collective-permute-done((f32[48,8,128]{2,1,0:T(8,128)S(1)}, f32[48,8,128]{2,1,0:T(8,128)S(1)}, u32[]{:S(2)}, u32[]{:S(2)}) %collective-permute-start.3) | collective-permute-done | bytes 196640 | tf_op jit(solution)/shard_map/ppermute | solution.py:394
  25.4 0.1 shard_map.96
  25.5 3.0 %collective-permute-start.6 = (f32[48,8,128]{2,1,0:T(8,128)S(1)}, f32[48,8,128]{2,1,0:T(8,128)S(1)}, u32[]{:S(2)}, u32[]{:S(2)}) collective-permute-start(f32[48,8,128]{2,1,0:T(8,128)S(1)} %get-tuple-element.42), channel_id=1, source_target_pairs={{8,16},{16,8},{24,32},{32,24},{40,48},{48,40},{56,64},{64,56},{72,... | collective-permute-start | bytes 589832 | tf_op jit(solution)/shard_map/ppermute | solution.py:384
  28.5 5.8 %collective-permute-start.4 = (f32[288,128]{1,0:T(8,128)S(1)}, f32[288,128]{1,0:T(8,128)S(1)}, u32[]{:S(2)}, u32[]{:S(2)}) collective-permute-start(f32[288,128]{1,0:T(8,128)S(1)} %get-tuple-element.38), channel_id=1, source_target_pairs={{0,8},{8,0},{16,24},{24,16},{32,40},{40,32},{48,56},{56,48},{64,72... | collective-permute-start | bytes 442376 | tf_op jit(solution)/shard_map/ppermute | solution.py:384
  34.4 1.9 %collective-permute-start.5 = (f32[96,128]{1,0:T(8,128)S(1)}, f32[96,128]{1,0:T(8,128)S(1)}, u32[]{:S(2)}, u32[]{:S(2)}) collective-permute-start(f32[96,128]{1,0:T(8,128)S(1)} %get-tuple-element.41), channel_id=1, source_target_pairs={{0,8},{8,0},{16,24},{24,16},{32,40},{40,32},{48,56},{56,48},{64,72... | collective-permute-start | bytes 147464 | tf_op jit(solution)/shard_map/ppermute | solution.py:384
  36.3 1.4 %shard_map.94 = (f32[3,8,8,2048]{3,2,1,0:T(8,128)}, f32[48,8,128]{2,1,0:T(8,128)S(1)}, f32[48,8,128]{2,1,0:T(8,128)S(1)}) custom-call(f32[48,64,128]{2,1,0:T(8,128)S(1)} %shard_map.92.local_ref, f32[8,128]{1,0:T(8,128)S(1)} %collective-permute-done.za_ref, f32[8,128]{1,0:T(8,128)S(1)} %collective-permute-done.1.zb_ref, ...), custom_call_target="tpu_custom_call" | custom-call | flops 1000000 | bytes 1000000 | tf_op jit(solution)/shard_map/pallas_call | solution.py:448
  37.7 3.1 %collective-permute-done.4.ia_ref = f32[288,128]{1,0:T(8,128)S(1)} collective-permute-done((f32[288,128]{1,0:T(8,128)S(1)}, f32[288,128]{1,0:T(8,128)S(1)}, u32[]{:S(2)}, u32[]{:S(2)}) %collective-permute-start.4) | collective-permute-done | bytes 147488 | tf_op jit(solution)/shard_map/ppermute | solution.py:384
  40.8 0.5 %collective-permute-done.5.ea_ref = f32[96,128]{1,0:T(8,128)S(1)} collective-permute-done((f32[96,128]{1,0:T(8,128)S(1)}, f32[96,128]{1,0:T(8,128)S(1)}, u32[]{:S(2)}, u32[]{:S(2)}) %collective-permute-start.5) | collective-permute-done | bytes 49184 | tf_op jit(solution)/shard_map/ppermute | solution.py:384
  41.3 0.0 collective-permute-done.6.yb_ref
  41.3 0.8 %shard_map.97 = f32[3,8,8,2048]{3,2,1,0:T(8,128)} custom-call(f32[3,8,8,2048]{3,2,1,0:T(8,128)} %get-tuple-element.35.base_hbm, f32[48,8,128]{2,1,0:T(8,128)S(1)} %get-tuple-element.36.first_ref, f32[48,8,128]{2,1,0:T(8,128)S(1)} %get-tuple-element.37.last_ref, f32[288,128]{1,0:T(8,128)S(1)} %collective-permute-done.4.ia_ref, ...), custom_call_target="tpu_custom_call", output_to_operand_aliasing={{}: (0, {})} | custom-call | flops 1000000 | bytes 1000000 | tf_op jit(solution)/shard_map/pallas_call | solution.py:458
  (1 shorter events, 0.0 us)
Async XLA Ops:
  1.8 6.0 %collective-permute-start = (f32[8,128]{1,0:T(8,128)S(1)}, f32[8,128]{1,0:T(8,128)S(1)}, u32[]{:S(2)}, u32[]{:S(2)}) collective-permute-start(f32[8,128]{1,0:T(8,128)S(1)} %get-tuple-element.31), channel_id=1, source_target_pairs={{0,1},{1,0},{2,3},{3,2},{4,5},{5,4},{6,7},{7,6},{8,9},{9,8},{10,11... | collective-permute-start | bytes 12296 | tf_op jit(solution)/shard_map/ppermute | solution.py:384
  3.8 4.1 %collective-permute-start.1 = (f32[8,128]{1,0:T(8,128)S(1)}, f32[8,128]{1,0:T(8,128)S(1)}, u32[]{:S(2)}, u32[]{:S(2)}) collective-permute-start(f32[8,128]{1,0:T(8,128)S(1)} %get-tuple-element.32), channel_id=1, source_target_pairs={{1,2},{2,1},{3,4},{4,3},{5,6},{6,5},{9,10},{10,9},{11,12},{12,11},... | collective-permute-start | bytes 12296 | tf_op jit(solution)/shard_map/ppermute | solution.py:384
  8.0 8.6 %collective-permute-start.2 = (f32[48,8,128]{2,1,0:T(8,128)S(1)}, f32[48,8,128]{2,1,0:T(8,128)S(1)}, u32[]{:S(2)}, u32[]{:S(2)}) collective-permute-start(f32[48,8,128]{2,1,0:T(8,128)S(1)} %get-tuple-element.33), channel_id=1, source_target_pairs={{0,128},{128,0},{256,384},{384,256},{129,257},{257,129},{2,130},{1... | collective-permute-start | bytes 589832 | tf_op jit(solution)/shard_map/ppermute | solution.py:394
  10.3 15.1 %collective-permute-start.3 = (f32[48,8,128]{2,1,0:T(8,128)S(1)}, f32[48,8,128]{2,1,0:T(8,128)S(1)}, u32[]{:S(2)}, u32[]{:S(2)}) collective-permute-start(f32[48,8,128]{2,1,0:T(8,128)S(1)} %get-tuple-element.34), channel_id=1, source_target_pairs={{128,256},{256,128},{1,129},{129,1},{257,385},{385,257},{130,258},... | collective-permute-start | bytes 589832 | tf_op jit(solution)/shard_map/ppermute | solution.py:394
  25.5 15.8 %collective-permute-start.6 = (f32[48,8,128]{2,1,0:T(8,128)S(1)}, f32[48,8,128]{2,1,0:T(8,128)S(1)}, u32[]{:S(2)}, u32[]{:S(2)}) collective-permute-start(f32[48,8,128]{2,1,0:T(8,128)S(1)} %get-tuple-element.42), channel_id=1, source_target_pairs={{8,16},{16,8},{24,32},{32,24},{40,48},{48,40},{56,64},{64,56},{72,... | collective-permute-start | bytes 589832 | tf_op jit(solution)/shard_map/ppermute | solution.py:384
  28.5 12.3 %collective-permute-start.4 = (f32[288,128]{1,0:T(8,128)S(1)}, f32[288,128]{1,0:T(8,128)S(1)}, u32[]{:S(2)}, u32[]{:S(2)}) collective-permute-start(f32[288,128]{1,0:T(8,128)S(1)} %get-tuple-element.38), channel_id=1, source_target_pairs={{0,8},{8,0},{16,24},{24,16},{32,40},{40,32},{48,56},{56,48},{64,72... | collective-permute-start | bytes 442376 | tf_op jit(solution)/shard_map/ppermute | solution.py:384
  34.4 6.9 %collective-permute-start.5 = (f32[96,128]{1,0:T(8,128)S(1)}, f32[96,128]{1,0:T(8,128)S(1)}, u32[]{:S(2)}, u32[]{:S(2)}) collective-permute-start(f32[96,128]{1,0:T(8,128)S(1)} %get-tuple-element.41), channel_id=1, source_target_pairs={{0,8},{8,0},{16,24},{24,16},{32,40},{40,32},{48,56},{56,48},{64,72... | collective-permute-start | bytes 147464 | tf_op jit(solution)/shard_map/ppermute | solution.py:384
where the time goes:
time: 42.4 us; the launch traced here: 42.1 us
  starting transfers between devices  21.8 us (51%)
  waiting for transfers between devices  12.5 us (29%)
  Pallas kernels  7.74 us (18%)
    ppermute x5, starting transfers between devices, exchange(): return lax.ppermute(array, axis, pairs_from(start, lax.axis_size(axis)))  13.4 us
    ppermute x2, waiting for transfers between devices, mixed_exchange(): return lax.ppermute(array, ('gx', 'gy', 'gz'), found)  8.89 us
    ppermute x2, starting transfers between devices, mixed_exchange(): return lax.ppermute(array, ('gx', 'gy', 'gz'), found)  8.4 us
    ppermute x5, waiting for transfers between devices, exchange(): return lax.ppermute(array, axis, pairs_from(start, lax.axis_size(axis)))  3.62 us
    pallas_call x1, Pallas kernels, local(): result, = call(stiffness_kernel, [flat])(*loaded[:-2])  3.4 us
    pallas_call x1, Pallas kernels, local(): call(load_kernel, [nodal.shape, (8 * blocks, BLOCK)] + kept + [tile, tile...  1.84 us
    pallas_call x1, Pallas kernels, local(): call(base_kernel, [nodal.shape, face, face], [pltpu.VMEM(nodal.shape, F32...  1.4 us
  transfers between devices with their start and end apart: 7, of which 4 were waited for; matrix products, arithmetic and copies ran while one was open for 0% of the time, Pallas kernels for 11%

commit v1 on v0

--- a/solution.py
+++ b/solution.py
@@ -252,7 +252,7 @@
 
 def parities():
     x, y, z = [lax.axis_index(axis) for axis in ("gx", "gy", "gz")]
-    return [lax.rem(index, 2) == 0 for index in (x + z, y, z)]
+    return [lax.rem(index, 2) == 0 for index in (x + z, y + z, z)]
 
 
 def at_lane(packed, slot, lane_to):
@@ -384,14 +384,13 @@
     return lax.ppermute(array, axis, pairs_from(start, lax.axis_size(axis)))
 
 
-def mixed_exchange(array, side):
-    width, height, depth = [lax.axis_size(axis) for axis in ("gx", "gy", "gz")]
+def mixed_exchange(array, axis, side):
+    depth = lax.axis_size("gz")
     found = []
-    for y in range(height):
-        for z in range(depth):
-            for i, j in pairs_from((side + z) % 2, width):
-                found.append(((i * height + y) * depth + z, (j * height + y) * depth + z))
-    return lax.ppermute(array, ("gx", "gy", "gz"), found)
+    for z in range(depth):
+        for i, j in pairs_from((side + z) % 2, lax.axis_size(axis)):
+            found.append((i * depth + z, j * depth + z))
+    return lax.ppermute(array, (axis, "gz"), found)
 
 
 def call(kernel, outs, scratch=(), flops=1000000, **specs):
@@ -437,13 +436,13 @@
         [face, face, inner, edge, face],
         [pltpu.VMEM((2 * components, 64, LANES), F32)],
     )(result, za, zb)
-    xa = mixed_exchange(xa, 0)
-    xb = mixed_exchange(xb, 1)
-    ia = exchange(ia, "gy", 0)
+    xa = mixed_exchange(xa, "gx", 0)
+    xb = mixed_exchange(xb, "gx", 1)
+    ia = mixed_exchange(ia, "gy", 0)
     (ea,) = call(copy_kernel, [edge])(ea)
     ea, yb = call(edge_kernel, [edge, face])(ea, yb, xa, xb)
-    yb = exchange(yb, "gy", 1)
-    ea = exchange(ea, "gy", 0)
+    yb = mixed_exchange(yb, "gy", 1)
+    ea = mixed_exchange(ea, "gy", 0)
     vmem = pl.BlockSpec(memory_space=pltpu.VMEM)
     result, first, last = call(
         base_kernel,

time: 42.4 us -> 42.7 us (level)
  the two profiles are of different devices: /device:TPU:208 before, /device:TPU:217 now
where the time goes in v1:
time: 42.7 us; the launch traced here: 42.4 us
  starting transfers between devices  22.3 us (52%)
  waiting for transfers between devices  12.3 us (29%)
  Pallas kernels  7.75 us (18%)
    ppermute x5, starting transfers between devices, mixed_exchange(): return lax.ppermute(array, (axis, 'gz'), found)  16.7 us
    ppermute x5, waiting for transfers between devices, mixed_exchange(): return lax.ppermute(array, (axis, 'gz'), found)  12.3 us
    ppermute x2, starting transfers between devices, exchange(): return lax.ppermute(array, axis, pairs_from(start, lax.axis_size(axis)))  5.6 us
    pallas_call x1, Pallas kernels, local(): result, = call(stiffness_kernel, [flat])(*loaded[:-2])  3.4 us
    pallas_call x1, Pallas kernels, local(): call(load_kernel, [nodal.shape, (8 * blocks, BLOCK)] + kept + [tile, tile...  1.84 us
    pallas_call x1, Pallas kernels, local(): call(base_kernel, [nodal.shape, face, face], [pltpu.VMEM(nodal.shape, F32...  1.4 us
  transfers between devices with their start and end apart: 7, of which 3 were waited for; matrix products, arithmetic and copies ran while one was open for 0% of the time, Pallas kernels for 11%

profile of v1, /device:TPU:217, one launch (start us, length us, event | category | flops | bytes accessed | tf_op | source)
XLA Modules:
  0.0 42.4 jit_solution(8415223714701524488)
XLA Ops:
  0.0 1.8 %shard_map.91 = (f32[3,8,8,2048]{3,2,1,0:T(8,128)S(1)}, f32[64,256]{1,0:T(8,128)S(1)}, bf16[128,192]{1,0:T(8,128)(2,1)S(1)}, bf16[128,256]{1,0:T(8,128)(2,1)S(1)...) custom-call(f32[3,8,8,2048]{3,2,1,0:T(8,128)} %u_hbm.1, ...), custom_call_target="tpu_custom_call" | custom-call | flops 1000000 | bytes 1000000 | tf_op jit(solution)/shard_map/pallas_call | solution.py:424
  1.8 2.6 %collective-permute-start = (f32[8,128]{1,0:T(8,128)S(1)}, f32[8,128]{1,0:T(8,128)S(1)}, u32[]{:S(2)}, u32[]{:S(2)}) collective-permute-start(f32[8,128]{1,0:T(8,128)S(1)} %get-tuple-element.31), channel_id=1, source_target_pairs={{0,1},{1,0},{2,3},{3,2},{4,5},{5,4},{6,7},{7,6},{8,9},{9,8},{10,11... | collective-permute-start | bytes 12296 | tf_op jit(solution)/shard_map/ppermute | solution.py:384
  4.4 3.0 %collective-permute-start.1 = (f32[8,128]{1,0:T(8,128)S(1)}, f32[8,128]{1,0:T(8,128)S(1)}, u32[]{:S(2)}, u32[]{:S(2)}) collective-permute-start(f32[8,128]{1,0:T(8,128)S(1)} %get-tuple-element.32), channel_id=1, source_target_pairs={{1,2},{2,1},{3,4},{4,3},{5,6},{6,5},{9,10},{10,9},{11,12},{12,11},... | collective-permute-start | bytes 12296 | tf_op jit(solution)/shard_map/ppermute | solution.py:384
  7.5 3.4 %shard_map.92.local_ref = f32[48,64,128]{2,1,0:T(8,128)S(1)} custom-call(f32[3,8,8,2048]{3,2,1,0:T(8,128)S(1)} %get-tuple-element.24.u_ref, f32[64,256]{1,0:T(8,128)S(1)} %get-tuple-element.25.factor_ref, bf16[128,192]{1,0:T(8,128)(2,1)S(1)} %get-tuple-element.26.gy_ref, bf16[128,256]{1,0:T(8,128)(2,1)S(1)} %get-tuple-element.27.by_ref, ...), custom_call_target="tpu_custom_call" | custom-call | flops 1000000 | bytes 1000000 | tf_op jit(solution)/shard_map/pallas_call | solution.py:433
  10.9 0.0 collective-permute-done.za_ref
  10.9 0.0 collective-permute-done.1.zb_ref
  10.9 0.2 shard_map.93
  11.1 4.5 %collective-permute-start.2 = (f32[48,8,128]{2,1,0:T(8,128)S(1)}, f32[48,8,128]{2,1,0:T(8,128)S(1)}, u32[]{:S(2)}, u32[]{:S(2)}) collective-permute-start(f32[48,8,128]{2,1,0:T(8,128)S(1)} %get-tuple-element.33), channel_id=1, source_target_pairs={{0,128},{128,0},{256,384},{384,256},{129,257},{257,129},{2,130},{1... | collective-permute-start | bytes 589832 | tf_op jit(solution)/shard_map/ppermute | solution.py:393
  15.6 1.9 %collective-permute-start.3 = (f32[48,8,128]{2,1,0:T(8,128)S(1)}, f32[48,8,128]{2,1,0:T(8,128)S(1)}, u32[]{:S(2)}, u32[]{:S(2)}) collective-permute-start(f32[48,8,128]{2,1,0:T(8,128)S(1)} %get-tuple-element.34), channel_id=1, source_target_pairs={{128,256},{256,128},{1,129},{129,1},{257,385},{385,257},{130,258},... | collective-permute-start | bytes 589832 | tf_op jit(solution)/shard_map/ppermute | solution.py:393
  17.5 8.2 %collective-permute-done.2.xa_ref = f32[48,8,128]{2,1,0:T(8,128)S(1)} collective-permute-done((f32[48,8,128]{2,1,0:T(8,128)S(1)}, f32[48,8,128]{2,1,0:T(8,128)S(1)}, u32[]{:S(2)}, u32[]{:S(2)}) %collective-permute-start.2) | collective-permute-done | bytes 196640 | tf_op jit(solution)/shard_map/ppermute | solution.py:393
  25.7 0.0 collective-permute-done.3.xb_ref
  25.7 0.1 shard_map.96
  25.8 1.9 %collective-permute-start.6 = (f32[48,8,128]{2,1,0:T(8,128)S(1)}, f32[48,8,128]{2,1,0:T(8,128)S(1)}, u32[]{:S(2)}, u32[]{:S(2)}) collective-permute-start(f32[48,8,128]{2,1,0:T(8,128)S(1)} %get-tuple-element.42), channel_id=1, source_target_pairs={{8,16},{16,8},{24,32},{32,24},{40,48},{48,40},{56,64},{64,56},{72,... | collective-permute-start | bytes 589832 | tf_op jit(solution)/shard_map/ppermute | solution.py:393
  27.7 6.4 %collective-permute-start.4 = (f32[288,128]{1,0:T(8,128)S(1)}, f32[288,128]{1,0:T(8,128)S(1)}, u32[]{:S(2)}, u32[]{:S(2)}) collective-permute-start(f32[288,128]{1,0:T(8,128)S(1)} %get-tuple-element.38), channel_id=1, source_target_pairs={{0,8},{8,0},{16,24},{24,16},{32,40},{40,32},{48,56},{56,48},{64,72... | collective-permute-start | bytes 442376 | tf_op jit(solution)/shard_map/ppermute | solution.py:393
  34.1 1.9 %collective-permute-start.5 = (f32[96,128]{1,0:T(8,128)S(1)}, f32[96,128]{1,0:T(8,128)S(1)}, u32[]{:S(2)}, u32[]{:S(2)}) collective-permute-start(f32[96,128]{1,0:T(8,128)S(1)} %get-tuple-element.41), channel_id=1, source_target_pairs={{0,8},{8,0},{16,24},{24,16},{32,40},{40,32},{48,56},{56,48},{64,72... | collective-permute-start | bytes 147464 | tf_op jit(solution)/shard_map/ppermute | solution.py:393
  36.1 1.4 %shard_map.94 = (f32[3,8,8,2048]{3,2,1,0:T(8,128)}, f32[48,8,128]{2,1,0:T(8,128)S(1)}, f32[48,8,128]{2,1,0:T(8,128)S(1)}) custom-call(f32[48,64,128]{2,1,0:T(8,128)S(1)} %shard_map.92.local_ref, f32[8,128]{1,0:T(8,128)S(1)} %collective-permute-done.za_ref, f32[8,128]{1,0:T(8,128)S(1)} %collective-permute-done.1.zb_ref, ...), custom_call_target="tpu_custom_call" | custom-call | flops 1000000 | bytes 1000000 | tf_op jit(solution)/shard_map/pallas_call | solution.py:447
  37.5 2.7 %collective-permute-done.4.ia_ref = f32[288,128]{1,0:T(8,128)S(1)} collective-permute-done((f32[288,128]{1,0:T(8,128)S(1)}, f32[288,128]{1,0:T(8,128)S(1)}, u32[]{:S(2)}, u32[]{:S(2)}) %collective-permute-start.4) | collective-permute-done | bytes 147488 | tf_op jit(solution)/shard_map/ppermute | solution.py:393
  40.2 1.4 %collective-permute-done.5.ea_ref = f32[96,128]{1,0:T(8,128)S(1)} collective-permute-done((f32[96,128]{1,0:T(8,128)S(1)}, f32[96,128]{1,0:T(8,128)S(1)}, u32[]{:S(2)}, u32[]{:S(2)}) %collective-permute-start.5) | collective-permute-done | bytes 49184 | tf_op jit(solution)/shard_map/ppermute | solution.py:393
  41.6 0.0 collective-permute-done.6.yb_ref
  41.6 0.8 %shard_map.97 = f32[3,8,8,2048]{3,2,1,0:T(8,128)} custom-call(f32[3,8,8,2048]{3,2,1,0:T(8,128)} %get-tuple-element.35.base_hbm, f32[48,8,128]{2,1,0:T(8,128)S(1)} %get-tuple-element.36.first_ref, f32[48,8,128]{2,1,0:T(8,128)S(1)} %get-tuple-element.37.last_ref, f32[288,128]{1,0:T(8,128)S(1)} %collective-permute-done.4.ia_ref, ...), custom_call_target="tpu_custom_call", output_to_operand_aliasing={{}: (0, {})} | custom-call | flops 1000000 | bytes 1000000 | tf_op jit(solution)/shard_map/pallas_call | solution.py:457
  (1 shorter events, 0.0 us)
Async XLA Ops:
  1.8 9.0 %collective-permute-start = (f32[8,128]{1,0:T(8,128)S(1)}, f32[8,128]{1,0:T(8,128)S(1)}, u32[]{:S(2)}, u32[]{:S(2)}) collective-permute-start(f32[8,128]{1,0:T(8,128)S(1)} %get-tuple-element.31), channel_id=1, source_target_pairs={{0,1},{1,0},{2,3},{3,2},{4,5},{5,4},{6,7},{7,6},{8,9},{9,8},{10,11... | collective-permute-start | bytes 12296 | tf_op jit(solution)/shard_map/ppermute | solution.py:384
  4.4 6.4 %collective-permute-start.1 = (f32[8,128]{1,0:T(8,128)S(1)}, f32[8,128]{1,0:T(8,128)S(1)}, u32[]{:S(2)}, u32[]{:S(2)}) collective-permute-start(f32[8,128]{1,0:T(8,128)S(1)} %get-tuple-element.32), channel_id=1, source_target_pairs={{1,2},{2,1},{3,4},{4,3},{5,6},{6,5},{9,10},{10,9},{11,12},{12,11},... | collective-permute-start | bytes 12296 | tf_op jit(solution)/shard_map/ppermute | solution.py:384
  11.1 14.6 %collective-permute-start.2 = (f32[48,8,128]{2,1,0:T(8,128)S(1)}, f32[48,8,128]{2,1,0:T(8,128)S(1)}, u32[]{:S(2)}, u32[]{:S(2)}) collective-permute-start(f32[48,8,128]{2,1,0:T(8,128)S(1)} %get-tuple-element.33), channel_id=1, source_target_pairs={{0,128},{128,0},{256,384},{384,256},{129,257},{257,129},{2,130},{1... | collective-permute-start | bytes 589832 | tf_op jit(solution)/shard_map/ppermute | solution.py:393
  15.6 10.1 %collective-permute-start.3 = (f32[48,8,128]{2,1,0:T(8,128)S(1)}, f32[48,8,128]{2,1,0:T(8,128)S(1)}, u32[]{:S(2)}, u32[]{:S(2)}) collective-permute-start(f32[48,8,128]{2,1,0:T(8,128)S(1)} %get-tuple-element.34), channel_id=1, source_target_pairs={{128,256},{256,128},{1,129},{129,1},{257,385},{385,257},{130,258},... | collective-permute-start | bytes 589832 | tf_op jit(solution)/shard_map/ppermute | solution.py:393
  25.8 15.8 %collective-permute-start.6 = (f32[48,8,128]{2,1,0:T(8,128)S(1)}, f32[48,8,128]{2,1,0:T(8,128)S(1)}, u32[]{:S(2)}, u32[]{:S(2)}) collective-permute-start(f32[48,8,128]{2,1,0:T(8,128)S(1)} %get-tuple-element.42), channel_id=1, source_target_pairs={{8,16},{16,8},{24,32},{32,24},{40,48},{48,40},{56,64},{64,56},{72,... | collective-permute-start | bytes 589832 | tf_op jit(solution)/shard_map/ppermute | solution.py:393
  27.7 12.5 %collective-permute-start.4 = (f32[288,128]{1,0:T(8,128)S(1)}, f32[288,128]{1,0:T(8,128)S(1)}, u32[]{:S(2)}, u32[]{:S(2)}) collective-permute-start(f32[288,128]{1,0:T(8,128)S(1)} %get-tuple-element.38), channel_id=1, source_target_pairs={{0,8},{8,0},{16,24},{24,16},{32,40},{40,32},{48,56},{56,48},{64,72... | collective-permute-start | bytes 442376 | tf_op jit(solution)/shard_map/ppermute | solution.py:393
  34.1 7.4 %collective-permute-start.5 = (f32[96,128]{1,0:T(8,128)S(1)}, f32[96,128]{1,0:T(8,128)S(1)}, u32[]{:S(2)}, u32[]{:S(2)}) collective-permute-start(f32[96,128]{1,0:T(8,128)S(1)} %get-tuple-element.41), channel_id=1, source_target_pairs={{0,8},{8,0},{16,24},{24,16},{32,40},{40,32},{48,56},{56,48},{64,72... | collective-permute-start | bytes 147464 | tf_op jit(solution)/shard_map/ppermute | solution.py:393
